TPU v7x, 512 devices: a whole 4x4x16 slice. The times are simulated.
512 devices in a mesh: tm: 128 (over z, x, core), space: 4 (over y).
Axes of the slice: x: 4, y: 4, z: 16, core: 2. Of those that a mesh axis runs over, the one named last changes fastest.
Arguments:
- state: float32 [512, 16, 64, 128], P('tm', 'space'), may hold values from -6 to 6
- source: float32 [512, 16, 64, 128], P('tm', 'space'), may hold values from -6 to 6
- absorption: float32 [16, 64, 128], P('space'), may hold values from 0.05 to 0.5
Outputs:
- relaxed: float32 [512, 16, 64, 128], P('tm', 'space')
- coarse_residual: float32 [128, 16, 64, 128], P('tm', 'space')
- residual_norm: float32 [], replicated
All inputs are finite; a program needn't handle non-finite values.
Results may differ from a plain program's by a relative error of at most 0.0004.
Values sent between devices are 32-bit elements; how exact they have to be, the bound alone decides.
A program may use at most 64 MiB of HBM per device.

v0:
```python
import math
import jax
import jax.numpy as jnp
from jax import lax
from jax.sharding import Mesh
from jax.sharding import PartitionSpec as P

CF = 4
SWEEPS = 5
TM = ("tm_0", "tm_1", "tm_2")
TM_SPACE = ("tm_0", "tm_1", "tm_2", "space")
coupling = 4.0


def shifted(value, axis, by):
    count = lax.axis_size(axis)
    pairs = [(i, i + by) for i in range(count) if 0 <= i + by < count]
    return lax.ppermute(value, axis, pairs)


def laid_out(tiles, dim):
    shape = list(tiles.shape[1:])
    shape[dim] *= tiles.shape[0]
    return jnp.moveaxis(tiles, 0, dim).reshape(shape)


def sent_to_all(value, axis):
    count = lax.axis_size(axis)
    return lax.all_to_all(
        jnp.broadcast_to(value[None], (count, *value.shape)), axis, 0, 0, tiled=True
    )


def collect(value, axis, dim):
    return laid_out(sent_to_all(value, axis), dim)


def by_axis(value, axes):
    for axis in axes:
        value = lax.psum(value, axis)
    return value


def sweep_weights(count):
    spread = 6.0 * coupling / (1.0 + 6.0 * coupling)
    return [
        1.0 / (1.0 + spread * math.cos(math.pi * (2 * k + 1) / (2 * count))) for k in range(count)
    ]


def apply_inner(extended, diag):
    inner = extended[1:-1]
    sides = jnp.pad(inner, ((0, 0), (1, 1), (1, 1)))
    beside = extended[2:] + extended[:-2]
    beside = beside + sides[:, 2:, 1:-1] + sides[:, :-2, 1:-1]
    beside = beside + sides[:, 1:-1, 2:] + sides[:, 1:-1, :-2]
    return diag * inner - coupling * beside


def step_whole(rhs, diag_full):
    field = rhs / diag_full
    for weight in sweep_weights(SWEEPS):
        extended = jnp.pad(field, ((1, 1), (0, 0), (0, 0)))
        field = field + weight * (rhs - apply_inner(extended, diag_full)) / diag_full
    return field


def local(state, source, absorption):
    depth_cells = absorption.shape[0]
    offset = lax.axis_index("space") * depth_cells

    def previous(last):
        return shifted(last, TM, 1)

    stacked = jnp.concatenate([state[:1], source, absorption[None]], axis=0)
    gathered = collect(stacked, "space", 1)
    source_full = gathered[1 : CF + 1]
    diag_full = 1.0 + 6.0 * coupling + gathered[CF + 1]

    def own_layers(field):
        return lax.dynamic_slice_in_dim(field, offset, depth_cells, 0)

    def back_full(last):
        return collect(previous(own_layers(last)), "space", 0)

    points = [gathered[0]] + [None] * (CF - 1)

    def relax_full(points):
        for j in range(1, CF):
            points[j] = step_whole(points[j - 1], diag_full) + source_full[j]
        return points

    points = relax_full(points)
    points[0] = step_whole(back_full(points[-1]), diag_full) + source_full[0]
    points = relax_full(points)
    coarse_full = source_full[0] + step_whole(back_full(points[-1]), diag_full) - points[0]
    coarse_residual = own_layers(coarse_full)
    points = [own_layers(point) for point in points]
    residual_norm = by_axis(jnp.sum(coarse_residual * coarse_residual), TM_SPACE)
    relaxed = jnp.stack(points, axis=0)
    return (relaxed, coarse_residual[None], residual_norm)


def solution(mesh):
    finer = Mesh(
        mesh.devices.reshape(16, 4, 2, mesh.shape["space"]), ("tm_0", "tm_1", "tm_2", "space")
    )
    return jax.shard_map(
        local,
        mesh=finer,
        in_specs=(P(TM, "space", None, None), P(TM, "space", None, None), P("space", None, None)),
        out_specs=(P(TM, "space", None, None), P(TM, "space", None, None), P()),
        check_vma=False,
    )
```

profile of v0, /device:TPU:2, one launch (start us, length us, event | category | flops | bytes accessed | tf_op | source)
XLA Modules:
  0.0 163.6 jit_solution(5410816493156166296)
XLA Ops:
  0.6 0.9 slice.797
  1.5 1.2 pad_maximum_fusion
  2.7 2.1 %broadcast_in_dim.11 = f32[4,6,4,64,128]{4,3,2,1,0:T(8,128)} broadcast(f32[6,4,64,128]{3,2,1,0:T(8,128)S(1)} %pad_maximum_fusion), dimensions={1,2,3,4} | broadcast | bytes 3932160 | tf_op jit(solution)/shard_map/broadcast_in_dim | solution.py:30
  4.8 4.5 %all-to-all-start = ((f32[4,6,4,64,128]{4,3,2,1,0:T(8,128)}), f32[4,6,4,64,128]{4,3,2,1,0:T(8,128)S(1)}, u32[]{:S(2)}, u32[]{:S(2)}) async-start(f32[4,6,4,64,128]{4,3,2,1,0:T(8,128)} %broadcast_in_dim.11), calls=%async_computation | async-start | bytes 6291456 | tf_op jit(solution)/shard_map/all_to_all | solution.py:29
  9.2 37.6 %all-to-all-done = f32[4,6,4,64,128]{4,3,2,1,0:T(8,128)S(1)} async-done(((f32[4,6,4,64,128]{4,3,2,1,0:T(8,128)}), f32[4,6,4,64,128]{4,3,2,1,0:T(8,128)S(1)}, u32[]{:S(2)}, u32[]{:S(2)}) %all-to-all-start) | async-done | bytes 3145760 | tf_op jit(solution)/shard_map/all_to_all | solution.py:29
  49.1 0.5 bitcast_divide_fusion.7
  50.4 0.4 fusion.86
  51.3 0.5 bitcast_divide_fusion.5
  52.6 0.4 fusion.141
  53.0 0.5 bitcast_multiply_fusion
  53.9 1.9 %collective-permute-start = (f32[4,64,128]{2,1,0:T(8,128)S(1)}, f32[4,64,128]{2,1,0:T(8,128)S(1)}, u32[]{:S(2)}, u32[]{:S(2)}) collective-permute-start(f32[4,64,128]{2,1,0:T(8,128)S(1)} %fusion.430), channel_id=1, source_target_pairs={{0,4},{4,8},{8,12},{12,16},{16,20},{20,24},{24,28},{28,32},{32,36}... | collective-permute-start | bytes 393224 | tf_op jit(solution)/shard_map/ppermute | solution.py:18
  55.8 4.4 %collective-permute-done = f32[4,64,128]{2,1,0:T(8,128)S(1)} collective-permute-done((f32[4,64,128]{2,1,0:T(8,128)S(1)}, f32[4,64,128]{2,1,0:T(8,128)S(1)}, u32[]{:S(2)}, u32[]{:S(2)}) %collective-permute-start) | collective-permute-done | bytes 131104 | tf_op jit(solution)/shard_map/ppermute | solution.py:18
  60.2 11.5 %all_to_all.15 = f32[4,4,64,128]{3,2,1,0:T(8,128)S(1)} all-to-all(f32[4,4,64,128]{3,2,1,0:T(8,128)S(1)} %broadcast_in_dim.12), channel_id=1, replica_groups=mesh['tm_0'=16,'tm_1'=4,'tm_2'=2,'space'=4] {'space'}, dimensions={0} | all-to-all | bytes 1048576 | tf_op jit(solution)/shard_map/all_to_all | solution.py:29
  73.6 0.5 bitcast_divide_fusion.3
  74.9 0.4 fusion.245
  75.8 0.4 bitcast_divide_fusion.6
  77.9 0.4 bitcast_divide_fusion.4
  79.3 0.4 fusion.355
  79.7 0.5 bitcast_multiply_fusion.1
  80.6 1.9 %collective-permute-start.1 = (f32[4,64,128]{2,1,0:T(8,128)S(1)}, f32[4,64,128]{2,1,0:T(8,128)S(1)}, u32[]{:S(2)}, u32[]{:S(2)}) collective-permute-start(f32[4,64,128]{2,1,0:T(8,128)S(1)} %get-tuple-element.27), channel_id=1, source_target_pairs={{0,4},{4,8},{8,12},{12,16},{16,20},{20,24},{24,28},{28,32},{32,36}... | collective-permute-start | bytes 393224 | tf_op jit(solution)/shard_map/ppermute | solution.py:18
  82.5 4.4 %collective-permute-done.1 = f32[4,64,128]{2,1,0:T(8,128)S(1)} collective-permute-done((f32[4,64,128]{2,1,0:T(8,128)S(1)}, f32[4,64,128]{2,1,0:T(8,128)S(1)}, u32[]{:S(2)}, u32[]{:S(2)}) %collective-permute-start.1) | collective-permute-done | bytes 131104 | tf_op jit(solution)/shard_map/ppermute | solution.py:18
  86.9 11.2 %all_to_all.16 = f32[4,4,64,128]{3,2,1,0:T(8,128)S(1)} all-to-all(f32[4,4,64,128]{3,2,1,0:T(8,128)S(1)} %broadcast_in_dim.13), channel_id=1, replica_groups=mesh['tm_0'=16,'tm_1'=4,'tm_2'=2,'space'=4] {'space'}, dimensions={0} | all-to-all | bytes 1048576 | tf_op jit(solution)/shard_map/all_to_all | solution.py:29
  98.2 0.4 fusion.383
  98.7 0.4 fusion.394
  99.1 0.4 fusion.404
  99.6 0.4 fusion.415
  100.4 1.3 multiply_reduce_fusion
  101.7 37.1 %psum.28 = f32[]{:T(128)} all-reduce(f32[]{:T(128)} %get-tuple-element.3), channel_id=1, replica_groups=mesh['tm_0'=16,'tm_1'=4,'tm_2'=2,'space'=4] {'tm_0'}, use_global_device_ids=true, to_apply=%region_1.2 | all-reduce | flops 1 | bytes 8 | tf_op jit(solution)/shard_map/psum | solution.py:40
  138.8 11.4 %psum.29 = f32[]{:T(128)} all-reduce(f32[]{:T(128)} %psum.28), channel_id=1, replica_groups=mesh['tm_0'=16,'tm_1'=4,'tm_2'=2,'space'=4] {'tm_1'}, use_global_device_ids=true, to_apply=%region_2.3 | all-reduce | flops 1 | bytes 8 | tf_op jit(solution)/shard_map/psum | solution.py:40
  150.2 3.1 %psum.30 = f32[]{:T(128)} all-reduce(f32[]{:T(128)} %psum.29), channel_id=1, replica_groups=mesh['tm_0'=16,'tm_1'=4,'tm_2'=2,'space'=4] {'tm_2'}, use_global_device_ids=true, to_apply=%region_3.4 | all-reduce | flops 1 | bytes 8 | tf_op jit(solution)/shard_map/psum | solution.py:40
  153.3 9.5 %psum.31 = f32[]{:T(128)} all-reduce(f32[]{:T(128)} %psum.30), channel_id=1, replica_groups=mesh['tm_0'=16,'tm_1'=4,'tm_2'=2,'space'=4] {'space'}, use_global_device_ids=true, to_apply=%region_4.5 | all-reduce | flops 1 | bytes 8 | tf_op jit(solution)/shard_map/psum | solution.py:40
  162.8 0.8 pad_maximum_fusion.1
  (34 shorter events, 11.3 us)
Async XLA Ops:
  4.8 42.0 %all-to-all-start = ((f32[4,6,4,64,128]{4,3,2,1,0:T(8,128)}), f32[4,6,4,64,128]{4,3,2,1,0:T(8,128)S(1)}, u32[]{:S(2)}, u32[]{:S(2)}) async-start(f32[4,6,4,64,128]{4,3,2,1,0:T(8,128)} %broadcast_in_dim.11), calls=%async_computation | async-start | bytes 6291456 | tf_op jit(solution)/shard_map/all_to_all | solution.py:29
  53.9 6.3 %collective-permute-start = (f32[4,64,128]{2,1,0:T(8,128)S(1)}, f32[4,64,128]{2,1,0:T(8,128)S(1)}, u32[]{:S(2)}, u32[]{:S(2)}) collective-permute-start(f32[4,64,128]{2,1,0:T(8,128)S(1)} %fusion.430), channel_id=1, source_target_pairs={{0,4},{4,8},{8,12},{12,16},{16,20},{20,24},{24,28},{28,32},{32,36}... | collective-permute-start | bytes 393224 | tf_op jit(solution)/shard_map/ppermute | solution.py:18
  80.6 6.3 %collective-permute-start.1 = (f32[4,64,128]{2,1,0:T(8,128)S(1)}, f32[4,64,128]{2,1,0:T(8,128)S(1)}, u32[]{:S(2)}, u32[]{:S(2)}) collective-permute-start(f32[4,64,128]{2,1,0:T(8,128)S(1)} %get-tuple-element.27), channel_id=1, source_target_pairs={{0,4},{4,8},{8,12},{12,16},{16,20},{20,24},{24,28},{28,32},{32,36}... | collective-permute-start | bytes 393224 | tf_op jit(solution)/shard_map/ppermute | solution.py:18
where the time goes:
time: 164 us
  blocking collectives  83.8 us (51%)
  waiting for transfers between devices  46.3 us (28%)
  other arithmetic  21.2 us (13%)
  starting transfers between devices  8.3 us (5%)
  local copies, waits for them, and re-layouts  3.06 us (2%)
    psum x4, blocking collectives, by_axis(): value = lax.psum(value, axis)  61.1 us
    all_to_all x1, waiting for transfers between devices, sent_to_all(): lax.all_to_all(jnp.broadcast_to(value[None], (count, *value.shape)), axis...  37.6 us
    all_to_all x2, blocking collectives, sent_to_all(): lax.all_to_all(jnp.broadcast_to(value[None], (count, *value.shape)), axis...  22.7 us
    add x30, other arithmetic, step_whole(): field + weight * (rhs - apply_inner(extended, diag_full)) / diag_full  12.9 us
    ppermute x2, waiting for transfers between devices, shifted(): return lax.ppermute(value, axis, pairs)  8.72 us
    all_to_all x1, starting transfers between devices, sent_to_all(): lax.all_to_all(jnp.broadcast_to(value[None], (count, *value.shape)), axis...  4.46 us
    ppermute x2, starting transfers between devices, shifted(): return lax.ppermute(value, axis, pairs)  3.84 us
  transfers between devices with their start and end apart: 3, of which 3 were waited for; matrix products, arithmetic and copies ran while one was open for 0% of the time, Pallas kernels for 0%

commit v1 on v0

--- a/solution.py
+++ b/solution.py
@@ -37,7 +37,7 @@
 
 def by_axis(value, axes):
     for axis in axes:
-        value = lax.psum(value, axis)
+        value = jnp.sum(lax.all_gather(value, axis), axis=0)
     return value
 
 

time: 164 us -> 176 us (1.073)
  blocking collectives: 83.8 us -> 70.1 us
  local copies, waits for them, and re-layouts: 3.06 us -> 14.6 us
  waiting for transfers between devices: 46.3 us -> 52.8 us
  other arithmetic: 21.2 us -> 25.2 us
  starting transfers between devices: 8.3 us -> 11.9 us
    psum x4 -> x0, blocking collectives: 61.1 us -> none  [by_axis(): value = lax.psum(value, axis)]
    unnamed x0 -> x4, blocking collectives: none -> 58.6 us
    all_to_all x2 -> x1, blocking collectives: 22.7 us -> 11.5 us  [sent_to_all(): lax.all_to_all(jnp.broadcast_to(value[None], (count, *value.shape)), axis...]
    unnamed x0 -> x12, local copies, waits for them, and re-layouts: none -> 10.7 us
    all_to_all x1 -> x2, waiting for transfers between devices: 37.6 us -> 44 us  [sent_to_all(): lax.all_to_all(jnp.broadcast_to(value[None], (count, *value.shape)), axis...]
    all_to_all x1 -> x2, starting transfers between devices: 4.46 us -> 8.11 us  [sent_to_all(): lax.all_to_all(jnp.broadcast_to(value[None], (count, *value.shape)), axis...]
    reduce_sum x0 -> x4, other arithmetic: none -> 2.41 us  [by_axis(): value = jnp.sum(lax.all_gather(value, axis), axis=0)]
  transfers between devices with their start and end apart: 3 -> 4, of which waited for: 3 -> 4; matrix products, arithmetic and copies ran while one was open for 0% -> 1% of each run, Pallas kernels for 0% -> 0%
where the time goes in v1:
time: 176 us
  blocking collectives  70.1 us (40%)
  waiting for transfers between devices  52.8 us (30%)
  other arithmetic  25.2 us (14%)
  local copies, waits for them, and re-layouts  14.6 us (8%)
  starting transfers between devices  11.9 us (7%)
    unnamed x4, blocking collectives  58.6 us
    all_to_all x2, waiting for transfers between devices, sent_to_all(): lax.all_to_all(jnp.broadcast_to(value[None], (count, *value.shape)), axis...  44 us
    add x30, other arithmetic, step_whole(): field + weight * (rhs - apply_inner(extended, diag_full)) / diag_full  12.8 us
    all_to_all x1, blocking collectives, sent_to_all(): lax.all_to_all(jnp.broadcast_to(value[None], (count, *value.shape)), axis...  11.5 us
    unnamed x12, local copies, waits for them, and re-layouts  10.7 us
    ppermute x2, waiting for transfers between devices, shifted(): return lax.ppermute(value, axis, pairs)  8.72 us
    all_to_all x2, starting transfers between devices, sent_to_all(): lax.all_to_all(jnp.broadcast_to(value[None], (count, *value.shape)), axis...  8.11 us
    ppermute x2, starting transfers between devices, shifted(): return lax.ppermute(value, axis, pairs)  3.84 us
  transfers between devices with their start and end apart: 4, of which 4 were waited for; matrix products, arithmetic and copies ran while one was open for 1% of the time, Pallas kernels for 0%

profile of v1, /device:TPU:2, one launch (start us, length us, event | category | flops | bytes accessed | tf_op | source)
XLA Modules:
  0.0 175.6 jit_solution(16651773811319763876)
XLA Ops:
  0.6 0.9 slice.797
  1.5 1.2 pad_maximum_fusion
  2.7 2.1 %broadcast_in_dim.11 = f32[4,6,4,64,128]{4,3,2,1,0:T(8,128)} broadcast(f32[6,4,64,128]{3,2,1,0:T(8,128)S(1)} %pad_maximum_fusion), dimensions={1,2,3,4} | broadcast | bytes 3932160 | tf_op jit(solution)/shard_map/broadcast_in_dim | solution.py:30
  4.8 4.6 %all-to-all-start = ((f32[4,6,4,64,128]{4,3,2,1,0:T(8,128)}), f32[4,6,4,64,128]{4,3,2,1,0:T(8,128)}, u32[]{:S(2)}, u32[]{:S(2)}) async-start(f32[4,6,4,64,128]{4,3,2,1,0:T(8,128)} %broadcast_in_dim.11), calls=%async_computation | async-start | bytes 6291456 | tf_op jit(solution)/shard_map/all_to_all | solution.py:29
  9.5 37.9 %all-to-all-done = f32[4,6,4,64,128]{4,3,2,1,0:T(8,128)} async-done(((f32[4,6,4,64,128]{4,3,2,1,0:T(8,128)}), f32[4,6,4,64,128]{4,3,2,1,0:T(8,128)}, u32[]{:S(2)}, u32[]{:S(2)}) %all-to-all-start) | async-done | bytes 3145760 | tf_op jit(solution)/shard_map/all_to_all | solution.py:29
  47.4 2.1 %fusion.441 = (f32[1,4,4,64,128]{4,3,2,0,1:T(8,128)S(1)}, f32[1,4,4,64,128]{4,3,2,0,1:T(8,128)S(1)}, f32[1,4,4,64,128]{4,3,2,0,1:T(8,128)S(1)}, f32[1,4,4,64,128...) fusion(f32[6,4,4,64,128]{4,3,2,0,1:T(8,128)} %bitcast.1), kind=kLoop, calls=%fused_computation.698 | loop fusion | flops 131072 | bytes 6291456 | tf_op jit(solution)/shard_map/slice | solution.py:90
  56.3 1.9 %collective-permute-start = (f32[4,64,128]{2,1,0:T(8,128)S(1)}, f32[4,64,128]{2,1,0:T(8,128)S(1)}, u32[]{:S(2)}, u32[]{:S(2)}) collective-permute-start(f32[4,64,128]{2,1,0:T(8,128)S(1)} %fusion.430), channel_id=1, source_target_pairs={{0,4},{4,8},{8,12},{12,16},{16,20},{20,24},{24,28},{28,32},{32,36}... | collective-permute-start | bytes 393224 | tf_op jit(solution)/shard_map/ppermute | solution.py:18
  58.2 4.4 %collective-permute-done = f32[4,64,128]{2,1,0:T(8,128)S(1)} collective-permute-done((f32[4,64,128]{2,1,0:T(8,128)S(1)}, f32[4,64,128]{2,1,0:T(8,128)S(1)}, u32[]{:S(2)}, u32[]{:S(2)}) %collective-permute-start) | collective-permute-done | bytes 131104 | tf_op jit(solution)/shard_map/ppermute | solution.py:18
  62.6 11.5 %all_to_all.15 = f32[4,4,64,128]{3,2,1,0:T(8,128)S(1)} all-to-all(f32[4,4,64,128]{3,2,1,0:T(8,128)S(1)} %broadcast_in_dim.12), channel_id=1, replica_groups=mesh['tm_0'=16,'tm_1'=4,'tm_2'=2,'space'=4] {'space'}, dimensions={0} | all-to-all | bytes 1048576 | tf_op jit(solution)/shard_map/all_to_all | solution.py:29
  82.8 1.9 %collective-permute-start.1 = (f32[4,64,128]{2,1,0:T(8,128)S(1)}, f32[4,64,128]{2,1,0:T(8,128)S(1)}, u32[]{:S(2)}, u32[]{:S(2)}) collective-permute-start(f32[4,64,128]{2,1,0:T(8,128)S(1)} %get-tuple-element.27), channel_id=1, source_target_pairs={{0,4},{4,8},{8,12},{12,16},{16,20},{20,24},{24,28},{28,32},{32,36}... | collective-permute-start | bytes 393224 | tf_op jit(solution)/shard_map/ppermute | solution.py:18
  84.8 4.4 %collective-permute-done.1 = f32[4,64,128]{2,1,0:T(8,128)S(1)} collective-permute-done((f32[4,64,128]{2,1,0:T(8,128)S(1)}, f32[4,64,128]{2,1,0:T(8,128)S(1)}, u32[]{:S(2)}, u32[]{:S(2)}) %collective-permute-start.1) | collective-permute-done | bytes 131104 | tf_op jit(solution)/shard_map/ppermute | solution.py:18
  89.1 0.8 broadcast_in_dim.13
  90.0 3.5 %all-to-all-start.2 = ((f32[4,4,64,128]{3,2,1,0:T(8,128)}), f32[4,4,64,128]{3,2,1,0:T(8,128)S(1)}, u32[]{:S(2)}, u32[]{:S(2)}) async-start(f32[4,4,64,128]{3,2,1,0:T(8,128)} %broadcast_in_dim.13), calls=%async_computation.2 | async-start | bytes 1048576 | tf_op jit(solution)/shard_map/all_to_all | solution.py:29
  93.4 1.3 dynamic-slice
  94.8 1.3 dynamic-slice.1
  96.1 6.1 %all-to-all-done.2 = f32[4,4,64,128]{3,2,1,0:T(8,128)S(1)} async-done(((f32[4,4,64,128]{3,2,1,0:T(8,128)}), f32[4,4,64,128]{3,2,1,0:T(8,128)S(1)}, u32[]{:S(2)}, u32[]{:S(2)}) %all-to-all-start.2) | async-done | bytes 524320 | tf_op jit(solution)/shard_map/all_to_all | solution.py:29
  104.4 1.3 multiply_reduce_fusion
  105.7 1.4 dynamic-update-slice
  107.1 36.5 %all-reduce.80 = f32[16]{0:T(128)S(1)} all-reduce(f32[16]{0:T(128)S(1)} %dynamic-update-slice), channel_id=1, replica_groups=mesh['tm_0'=16,'tm_1'=4,'tm_2'=2,'space'=4] {'tm_0'}, use_global_device_ids=true, to_apply=%add.80 | all-reduce | flops 16 | bytes 128
  143.6 0.6 reduce_sum.46
  144.2 1.3 dynamic-update-slice.1
  145.5 1.3 dynamic-slice.2
  146.8 10.7 %all-reduce.81 = f32[4]{0:T(128)S(1)} all-reduce(f32[4]{0:T(128)S(1)} %dynamic-update-slice.1), channel_id=1, replica_groups=mesh['tm_0'=16,'tm_1'=4,'tm_2'=2,'space'=4] {'tm_1'}, use_global_device_ids=true, to_apply=%add.81 | all-reduce | flops 4 | bytes 32
  157.5 0.6 reduce_sum.47
  158.1 1.4 dynamic-update-slice.2
  159.5 1.3 dynamic-slice.3
  160.8 2.4 %all-reduce.82 = f32[2]{0:T(128)S(1)} all-reduce(f32[2]{0:T(128)S(1)} %dynamic-update-slice.2), channel_id=1, replica_groups=mesh['tm_0'=16,'tm_1'=4,'tm_2'=2,'space'=4] {'tm_2'}, use_global_device_ids=true, to_apply=%add.82 | all-reduce | flops 2 | bytes 16
  163.2 0.6 reduce_sum.48
  163.8 1.4 dynamic-update-slice.3
  165.3 8.9 %all-reduce.83 = f32[4]{0:T(128)S(1)} all-reduce(f32[4]{0:T(128)S(1)} %dynamic-update-slice.3), channel_id=1, replica_groups=mesh['tm_0'=16,'tm_1'=4,'tm_2'=2,'space'=4] {'space'}, use_global_device_ids=true, to_apply=%add.83 | all-reduce | flops 4 | bytes 32
  174.2 0.6 reduce_sum.49
  174.8 0.8 pad_maximum_fusion.1
  (51 shorter events, 17.4 us)
Async XLA Ops:
  4.8 42.5 %all-to-all-start = ((f32[4,6,4,64,128]{4,3,2,1,0:T(8,128)}), f32[4,6,4,64,128]{4,3,2,1,0:T(8,128)}, u32[]{:S(2)}, u32[]{:S(2)}) async-start(f32[4,6,4,64,128]{4,3,2,1,0:T(8,128)} %broadcast_in_dim.11), calls=%async_computation | async-start | bytes 6291456 | tf_op jit(solution)/shard_map/all_to_all | solution.py:29
  56.3 6.3 %collective-permute-start = (f32[4,64,128]{2,1,0:T(8,128)S(1)}, f32[4,64,128]{2,1,0:T(8,128)S(1)}, u32[]{:S(2)}, u32[]{:S(2)}) collective-permute-start(f32[4,64,128]{2,1,0:T(8,128)S(1)} %fusion.430), channel_id=1, source_target_pairs={{0,4},{4,8},{8,12},{12,16},{16,20},{20,24},{24,28},{28,32},{32,36}... | collective-permute-start | bytes 393224 | tf_op jit(solution)/shard_map/ppermute | solution.py:18
  82.8 6.3 %collective-permute-start.1 = (f32[4,64,128]{2,1,0:T(8,128)S(1)}, f32[4,64,128]{2,1,0:T(8,128)S(1)}, u32[]{:S(2)}, u32[]{:S(2)}) collective-permute-start(f32[4,64,128]{2,1,0:T(8,128)S(1)} %get-tuple-element.27), channel_id=1, source_target_pairs={{0,4},{4,8},{8,12},{12,16},{16,20},{20,24},{24,28},{28,32},{32,36}... | collective-permute-start | bytes 393224 | tf_op jit(solution)/shard_map/ppermute | solution.py:18
  90.0 12.2 %all-to-all-start.2 = ((f32[4,4,64,128]{3,2,1,0:T(8,128)}), f32[4,4,64,128]{3,2,1,0:T(8,128)S(1)}, u32[]{:S(2)}, u32[]{:S(2)}) async-start(f32[4,4,64,128]{3,2,1,0:T(8,128)} %broadcast_in_dim.13), calls=%async_computation.2 | async-start | bytes 1048576 | tf_op jit(solution)/shard_map/all_to_all | solution.py:29
